TPU v7x, 32 devices: a whole 2x2x4 slice. The times are simulated.
32 devices in a mesh: rep: 4 (over z), exp: 4 (over x, core), shard: 2 (over y).
Axes of the slice: x: 2, y: 2, z: 4, core: 2. Of those that a mesh axis runs over, the one named last changes fastest.
Arguments:
- tokens: bfloat16 [3584, 2048], P(('rep', 'exp', 'shard')), may hold values from -1.5 to 1.5
- routes: int32 [3584, 2], P(('rep', 'exp', 'shard')), may hold values from 0 to 3, all different within a row; in each aligned block of 112 rows (0 to 111, 112 to 223, ...) at most 63 rows name the same one
- gate_weight: bfloat16 [4, 2048, 7168], P('exp', None, 'shard'), may hold values from -0.125 to 0.125
- gate_cotangent: bfloat16 [4, 2016, 7168], P('exp', 'rep', 'shard'), may hold values from -0.75 to 0.75
Outputs:
- token_grad: bfloat16 [3584, 2048], P(('rep', 'exp', 'shard'))
- weight_grad: bfloat16 [4, 2048, 7168], P('exp', None, 'shard')
Inputs may be any that keep to these rules, and one draw needn't show every extreme that they name: `routes`: the two entries of a row differ. The rows of one device name one expert at most 63 times, and some device names some expert exactly 63 times.
All inputs are finite; a program needn't handle non-finite values.
Results may differ from a plain program's by a relative error of at most 0.015.
Values may be sent and summed in bfloat16 or wider, within the bound.
A program may use at most 128 MiB of HBM per device.

v0:
```python
import jax
import jax.numpy as jnp
from jax import lax
from jax.sharding import PartitionSpec as P


def slot_matrix(route_rows, experts, slot_cap):
    expert_ids = jnp.arange(experts, dtype=jnp.int32)
    onehot = (route_rows[:, :, None] == expert_ids[None, None, :]).astype(jnp.int32)
    flattened = onehot.reshape(-1, experts)
    before = jnp.cumsum(flattened, axis=0) - flattened
    position = jnp.sum(before * flattened, axis=1)
    target = jnp.sum(flattened * expert_ids[None, :], axis=1) * slot_cap + position
    slot_ids = jnp.arange(experts * slot_cap, dtype=jnp.int32)
    matches = (target[None, :] == slot_ids[:, None]).astype(jnp.int32)
    return matches.reshape(experts * slot_cap, -1, 2).sum(axis=2)


def body(tokens, routes, gate_weight, gate_cotangent):
    experts = lax.axis_size("exp")
    shards = lax.axis_size("shard")
    features = tokens.shape[1]
    cotangent = gate_cotangent[0]
    hidden = cotangent.shape[1]
    slot_cap = cotangent.shape[0] // (experts * shards)
    weight = gate_weight[0]
    blocks = cotangent.reshape(experts, shards, slot_cap, hidden)
    placing = slot_matrix(routes, experts, slot_cap).astype(jnp.bfloat16)
    outgoing = jnp.dot(placing, tokens, preferred_element_type=jnp.float32).astype(jnp.bfloat16)
    outgoing = outgoing.reshape(experts, slot_cap, features)
    contract_rows = (((0,), (0,)), ((), ()))
    copies = jnp.broadcast_to(outgoing[:, None], (experts, shards, slot_cap, features))
    copies = copies.reshape(experts * shards, slot_cap, features)
    arrived = lax.all_to_all(copies, ("exp", "shard"), split_axis=0, concat_axis=0, tiled=True)
    partial_grad = lax.dot_general(
        arrived.reshape(-1, features), cotangent, contract_rows, preferred_element_type=jnp.float32
    )
    weight_grad = lax.psum(partial_grad.astype(jnp.bfloat16), "rep")[None]
    ordered = jnp.swapaxes(blocks, 0, 1).reshape(-1, hidden)
    summed = lax.psum_scatter(
        lax.dot_general(
            ordered, weight, (((1,), (1,)), ((), ())), preferred_element_type=jnp.float32
        ).astype(jnp.bfloat16),
        "shard",
        scatter_dimension=0,
        tiled=True,
    )
    slot_grad = summed.reshape(experts, slot_cap, features)
    returned = lax.all_to_all(slot_grad, "exp", split_axis=0, concat_axis=0, tiled=True)
    token_grad = jnp.dot(
        placing.T, returned.reshape(-1, features), preferred_element_type=jnp.float32
    )
    return (token_grad.astype(jnp.bfloat16), weight_grad)


def solution(mesh):
    placed = (
        P(("rep", "exp", "shard"), None),
        P(("rep", "exp", "shard"), None),
        P("exp", None, "shard"),
        P("exp", "rep", "shard"),
    )
    return jax.shard_map(
        body,
        mesh=mesh,
        in_specs=placed,
        out_specs=(P(("rep", "exp", "shard"), None), P("exp", None, "shard")),
        check_vma=False,
    )
```

profile of v0, /device:TPU:0, one launch (start us, length us, event | category | flops | bytes accessed | tf_op | source)
XLA Modules:
  0.0 571.3 jit_solution(2415380312625847076)
XLA Ops:
  7.2 0.8 copy.16
  8.2 1.2 reduce-window.6
  10.2 0.5 convolution_convert_fusion.1
  10.7 0.3 broadcast_in_dim.6
  11.0 0.2 broadcast_in_dim.7
  11.2 30.7 %all_to_all.10 = bf16[8,63,2048]{2,1,0:T(8,128)(2,1)S(1)} all-to-all(bf16[8,63,2048]{2,1,0:T(8,128)(2,1)S(1)} %bitcast.29), channel_id=1, replica_groups=mesh['rep'=4,'exp'=4,'shard'=2] {'exp','shard'}, dimensions={0} | all-to-all | bytes 4128768 | tf_op jit(solution)/shard_map/all_to_all | solution.py:34
  41.9 2.0 reshape.61
  43.8 13.3 %fusion.3 = bf16[1,2048,3584]{2,1,0:T(8,128)(2,1)} fusion(bf16[504,2048]{1,0:T(8,128)(2,1)} %reshape.61, bf16[1,504,3584]{2,1,0:T(8,128)(2,1)} %param.7), kind=kOutput, calls=%fused_computation.3 | convolution fusion | flops 7406092288 | bytes 20357120 | tf_op jit(solution)/shard_map/dot_general | solution.py:35
  57.2 4.9 reshape_squeeze.3
  62.1 5.2 copy.20
  67.2 4.9 reshape.57
  72.2 13.0 %fusion.5 = bf16[504,2048]{1,0:T(8,128)(2,1)} fusion(bf16[504,3584]{1,0:T(8,128)(2,1)} %reshape.57, bf16[1,2048,3584]{2,1,0:T(8,128)(2,1)} %param.6), kind=kOutput, calls=%fused_computation.5 | convolution fusion | flops 7399784448 | bytes 20357120 | tf_op jit(solution)/shard_map/dot_general | solution.py:41
  85.2 28.6 %fusion = bf16[256,2048]{1,0:T(8,128)(2,1)S(1)} fusion(bf16[504,2048]{1,0:T(8,128)(2,1)} %fusion.5), kind=kCustom, calls=%all-reduce-scatter | all-reduce-scatter fusion | flops 1048577 | bytes 3113472
  113.8 3.6 collective-permute-start
  117.5 0.6 dynamic-slice.4
  118.7 0.2 collective-permute-done
  118.9 1.2 concatenate
  120.1 0.3 constant_dynamic-slice_fusion
  120.4 0.3 reshape.58
  120.7 17.6 %all_to_all.11 = bf16[4,63,2048]{2,1,0:T(8,128)(2,1)} all-to-all(bf16[4,63,2048]{2,1,0:T(8,128)(2,1)S(1)} %reshape.58), channel_id=1, replica_groups=mesh['rep'=4,'exp'=4,'shard'=2] {'exp'}, dimensions={0} | all-to-all | bytes 2064384 | tf_op jit(solution)/shard_map/all_to_all | solution.py:49
  138.3 1.5 reshape.59
  139.8 1.1 convolution_convert_fusion.2
  140.9 410.5 %all-reduce.5.cloned.1.call-done = bf16[1,2048,3584]{2,1,0:T(8,128)(2,1)} async-done(((bf16[1,2048,3584]{2,1,0:T(8,128)(2,1)}), bf16[1,2048,3584]{2,1,0:T(8,128)(2,1)}) %all-reduce.5.cloned.1.call-update) | async-done | bytes 14680080 | tf_op jit(solution)/shard_map/psum | solution.py:38
  551.3 13.2 %copy.25 = bf16[1,2048,3584]{2,1,0:T(8,128)(2,1)} copy(bf16[1,2048,3584]{2,1,0:T(8,128)(2,1)} %all-reduce.5.cloned.1.call-done) | data formatting | bytes 29360128
  (25 shorter events, 1.0 us)
Async XLA Ops:
  7.2 3.1 copy-start
  7.2 544.1 %all-reduce.5.cloned.1.call-start = ((), (), s32[]{:S(2)}) async-start(), calls=%async_computation.2 | async-start | bytes 29360128 | tf_op jit(solution)/shard_map/psum | solution.py:38
  72.2 45.3 %copy-start.2 = (u32[32]{0:T(128)S(1)}, u32[32]{0:T(128)}, u32[]{:S(2)}) copy-start(u32[32]{0:T(128)} %constant.19) | copy-start | bytes 388
  113.8 5.1 collective-permute-start
  551.3 13.2 %copy-start.1 = (bf16[112,2048]{1,0:T(8,128)(2,1)S(1)}, bf16[112,2048]{1,0:T(8,128)(2,1)}, u32[]{:S(2)}) copy-start(bf16[112,2048]{1,0:T(8,128)(2,1)} %param.4) | copy-start | bytes 1376260
Sparse Core Ops, SparseCore 0:
  57.3 493.9 all-reduce.4
where the time goes:
time: 572 us; the launch traced here: 571 us
  waiting for transfers between devices  411 us (72%)
  blocking collectives  76.8 us (13%)
  local copies, waits for them, and re-layouts  36 us (6%)
  matrix products  27.9 us (5%)
  between operations  14.8 us (3%)
    psum x1, waiting for transfers between devices, body(): weight_grad = lax.psum(partial_grad.astype(jnp.bfloat16), 'rep')[None]  410 us
    all_to_all x1, blocking collectives, body(): lax.all_to_all(copies, ('exp', 'shard'), split_axis=0, concat_axis=0, til...  30.7 us
    unnamed x1, blocking collectives  28.6 us
    all_to_all x1, blocking collectives, body(): lax.all_to_all(slot_grad, 'exp', split_axis=0, concat_axis=0, tiled=True)  17.6 us
    unnamed x13, local copies, waits for them, and re-layouts  16.1 us
    dot_general x1, matrix products, body(): lax.dot_general(arrived.reshape(-1, features), cotangent, contract_rows,...  13.3 us
    dot_general x1, matrix products, body(): lax.dot_general(ordered, weight, (((1,), (1,)), ((), ())), preferred_elem...  13 us
  transfers between devices with their start and end apart: 2, of which 2 were waited for; matrix products, arithmetic and copies ran while one was open for 11% of the time, Pallas kernels for 0%

commit v1 on v0

--- a/solution.py
+++ b/solution.py
@@ -1,6 +1,8 @@
 import jax
 import jax.numpy as jnp
 from jax import lax
+from jax.experimental import pallas as pl
+from jax.experimental.pallas import tpu as pltpu
 from jax.sharding import PartitionSpec as P
 
 
@@ -16,26 +18,81 @@
     return matches.reshape(experts * slot_cap, -1, 2).sum(axis=2)
 
 
+def grad_kernel(*refs):
+    rows_ref, cotangent_ref, out_ref = refs[0], refs[1], refs[-1]
+    total = None
+    for replica in range(rows_ref.shape[0]):
+        term = jnp.dot(rows_ref[replica], cotangent_ref[replica], preferred_element_type=jnp.float32)
+        total = term if total is None else total + term
+    out_ref[0] = total.astype(out_ref.dtype)
+
+
+def grad_columns(rows, cotangent, held, hidden, start, width):
+    replicas, features, depth = rows.shape
+    columns = cotangent.shape[2]
+    tall = 512
+    in_specs = [
+        pl.BlockSpec((replicas, tall, depth), lambda j, i: (0, i, 0)),
+        pl.BlockSpec((replicas, depth, width), lambda j, i: (0, 0, j)),
+    ]
+    operands = [rows, cotangent]
+    aliases = {}
+    if held is not None:
+        in_specs.append(pl.BlockSpec(memory_space=pl.ANY))
+        operands.append(held)
+        aliases = {2: 0}
+    first = start // width
+    return pl.pallas_call(
+        grad_kernel,
+        grid=(columns // width, features // tall),
+        in_specs=in_specs,
+        out_specs=pl.BlockSpec((1, tall, width), lambda j, i: (0, i, j + first)),
+        out_shape=jax.ShapeDtypeStruct((1, features, hidden), jnp.bfloat16),
+        input_output_aliases=aliases,
+        compiler_params=pltpu.CompilerParams(
+            dimension_semantics=("arbitrary", "arbitrary"), vmem_limit_bytes=56 * 2**20
+        ),
+        cost_estimate=pl.CostEstimate(
+            flops=2 * replicas * depth * features * columns,
+            bytes_accessed=2 * (replicas * depth * (features + columns) + features * columns),
+            transcendentals=0,
+        ),
+    )(*operands)
+
+
 def body(tokens, routes, gate_weight, gate_cotangent):
     experts = lax.axis_size("exp")
     shards = lax.axis_size("shard")
+    replicas = lax.axis_size("rep")
     features = tokens.shape[1]
     cotangent = gate_cotangent[0]
-    hidden = cotangent.shape[1]
-    slot_cap = cotangent.shape[0] // (experts * shards)
+    rows, hidden = cotangent.shape
+    slot_cap = rows // (experts * shards)
     weight = gate_weight[0]
+    units = hidden // 128
+    width = 128 * max(u for u in range(1, units + 1) if units % u == 0 and u <= max(1, units // 4))
+    split = hidden - width
+
+    all_tokens = lax.all_gather(tokens[None], "rep", axis=0, tiled=True)
+    all_routes = lax.all_gather(routes[None], "rep", axis=0, tiled=True)
+    first_part, all_tokens = lax.optimization_barrier((gate_cotangent[:, :, :split], all_tokens))
+    first_all = lax.all_gather(first_part, "rep", axis=0, tiled=True)
+    last_part, first_all = lax.optimization_barrier((gate_cotangent[:, :, split:], first_all))
+    last_all = lax.all_gather(last_part, "rep", axis=0, tiled=True)
+
+    placing_all = jax.vmap(lambda r: slot_matrix(r, experts, slot_cap))(all_routes).astype(jnp.bfloat16)
+    outgoing = lax.dot_general(
+        placing_all, all_tokens, (((2,), (1,)), ((0,), (0,))), preferred_element_type=jnp.float32
+    ).astype(jnp.bfloat16)
+    outgoing = outgoing.reshape(replicas, experts, slot_cap, features).swapaxes(0, 1)
+    copies = jnp.broadcast_to(outgoing[:, None], (experts, shards, replicas, slot_cap, features))
+    copies = copies.reshape(experts * shards, replicas, slot_cap, features)
+    arrived = lax.all_to_all(copies, ("exp", "shard"), split_axis=0, concat_axis=0, tiled=True)
+    gathered = arrived.swapaxes(0, 1).reshape(replicas, rows, features)
+    lifted = gathered.swapaxes(1, 2)
+
+    placing = slot_matrix(routes, experts, slot_cap).astype(jnp.bfloat16)
     blocks = cotangent.reshape(experts, shards, slot_cap, hidden)
-    placing = slot_matrix(routes, experts, slot_cap).astype(jnp.bfloat16)
-    outgoing = jnp.dot(placing, tokens, preferred_element_type=jnp.float32).astype(jnp.bfloat16)
-    outgoing = outgoing.reshape(experts, slot_cap, features)
-    contract_rows = (((0,), (0,)), ((), ()))
-    copies = jnp.broadcast_to(outgoing[:, None], (experts, shards, slot_cap, features))
-    copies = copies.reshape(experts * shards, slot_cap, features)
-    arrived = lax.all_to_all(copies, ("exp", "shard"), split_axis=0, concat_axis=0, tiled=True)
-    partial_grad = lax.dot_general(
-        arrived.reshape(-1, features), cotangent, contract_rows, preferred_element_type=jnp.float32
-    )
-    weight_grad = lax.psum(partial_grad.astype(jnp.bfloat16), "rep")[None]
     ordered = jnp.swapaxes(blocks, 0, 1).reshape(-1, hidden)
     summed = lax.psum_scatter(
         lax.dot_general(
@@ -49,8 +106,12 @@
     returned = lax.all_to_all(slot_grad, "exp", split_axis=0, concat_axis=0, tiled=True)
     token_grad = jnp.dot(
         placing.T, returned.reshape(-1, features), preferred_element_type=jnp.float32
-    )
-    return (token_grad.astype(jnp.bfloat16), weight_grad)
+    ).astype(jnp.bfloat16)
+
+    lifted, token_grad = lax.optimization_barrier((lifted, token_grad))
+    weight_grad = grad_columns(lifted, first_all, None, hidden, 0, width)
+    weight_grad = grad_columns(lifted, last_all, weight_grad, hidden, split, width)
+    return (token_grad, weight_grad)
 
 
 def solution(mesh):

time: 572 us -> 335 us (0.59)
  waiting for transfers between devices: 411 us -> 142 us
  Pallas kernels: 0 us -> 46.2 us
  blocking collectives: 76.8 us -> 38.2 us
  local copies, waits for them, and re-layouts: 36 us -> 58.2 us
  matrix products: 27.9 us -> 16.6 us
  starting transfers between devices: 3.66 us -> 11.2 us
    psum x1 -> x0, waiting for transfers between devices: 410 us -> none  [body(): weight_grad = lax.psum(partial_grad.astype(jnp.bfloat16), 'rep')[None]]
    all_gather x0 -> x3, waiting for transfers between devices: none -> 135 us  [the longest x1 79.3 us: body(): first_all = lax.all_gather(first_part, 'rep', axis=0, tiled=True)]
    all_to_all x2 -> x0, blocking collectives: 48.2 us -> none  [the longest x1 30.7 us: body(): lax.all_to_all(copies, ('exp', 'shard'), split_axis=0, concat_axis=0, til...]
    pallas_call x0 -> x2, Pallas kernels: none -> 46.2 us  [grad_columns(): pl.pallas_call(grad_kernel, grid=(columns // width, features // tall), in...]
    reshape x1 -> x2, local copies, waits for them, and re-layouts: 1.95 us -> 18.8 us  [the longest x1 13.7 us: body(): gathered = arrived.swapaxes(0, 1).reshape(replicas, rows, features)]
    unnamed x13 -> x12, local copies, waits for them, and re-layouts: 16.1 us -> 2.22 us
    dot_general x2 -> x1, matrix products: 13.7 us -> 3.31 us  [body(): lax.dot_general(placing_all, all_tokens, (((2,), (1,)), ((0,), (0,))), pr...]
    all_gather x0 -> x1, blocking collectives: none -> 9.98 us  [body(): all_routes = lax.all_gather(routes[None], 'rep', axis=0, tiled=True)]
  transfers between devices with their start and end apart: 2 -> 6, of which waited for: 2 -> 4; matrix products, arithmetic and copies ran while one was open for 11% -> 33% of each run, Pallas kernels for 0% -> 10%
where the time goes in v1:
time: 335 us; the launch traced here: 334 us
  waiting for transfers between devices  142 us (42%)
  local copies, waits for them, and re-layouts  58.2 us (17%)
  Pallas kernels  46.2 us (14%)
  blocking collectives  38.2 us (11%)
  matrix products  16.6 us (5%)
  between operations  14.6 us (4%)
  starting transfers between devices  11.2 us (3%)
  other arithmetic  6.71 us (2%)
    all_gather x1, waiting for transfers between devices, body(): first_all = lax.all_gather(first_part, 'rep', axis=0, tiled=True)  79.3 us
    pallas_call x2, Pallas kernels, grad_columns(): pl.pallas_call(grad_kernel, grid=(columns // width, features // tall), in...  46.2 us
    all_gather x1, waiting for transfers between devices, body(): all_tokens = lax.all_gather(tokens[None], 'rep', axis=0, tiled=True)  42.1 us
    unnamed x1, blocking collectives  28.2 us
    all_gather x1, waiting for transfers between devices, body(): last_all = lax.all_gather(last_part, 'rep', axis=0, tiled=True)  13.8 us
    reshape x1, local copies, waits for them, and re-layouts, body(): gathered = arrived.swapaxes(0, 1).reshape(replicas, rows, features)  13.7 us
    dot_general x1, matrix products, body(): lax.dot_general(ordered, weight, (((1,), (1,)), ((), ())), preferred_elem...  12.2 us
    all_gather x1, blocking collectives, body(): all_routes = lax.all_gather(routes[None], 'rep', axis=0, tiled=True)  9.98 us
  transfers between devices with their start and end apart: 6, of which 4 were waited for; matrix products, arithmetic and copies ran while one was open for 33% of the time, Pallas kernels for 10%

profile of v1, /device:TPU:0, one launch (start us, length us, event | category | flops | bytes accessed | tf_op | source)
XLA Modules:
  0.0 334.2 jit_solution(14428939723169542185)
XLA Ops:
  7.9 3.6 %slice.27 = bf16[1,504,2688]{2,1,0:T(8,128)(2,1)} slice(bf16[1,504,3584]{2,1,0:T(8,128)(2,1)} %param.7), slice={[0:1], [0:504], [0:2688]} | slice | bytes 5419008 | tf_op jit(solution)/shard_map/slice | solution.py:78
  11.5 42.1 %all-gather.11.cloned.1.call-done = bf16[448,2048]{1,0:T(8,128)(2,1)} async-done(((bf16[112,2048]{1,0:T(8,128)(2,1)}), bf16[448,2048]{1,0:T(8,128)(2,1)}) %all-gather.11.cloned.1.call-update) | async-done | bytes 1835024 | tf_op jit(solution)/shard_map/all_gather | solution.py:76
  53.7 4.9 %reshape_squeeze.3 = bf16[4,2,63,3584]{3,2,1,0:T(8,128)(2,1)} reshape(bf16[1,504,3584]{2,1,0:T(8,128)(2,1)} %param.7) | data formatting | bytes 7225344 | tf_op jit(solution)/shard_map/reshape;squeeze | solution.py:95
  58.6 4.3 %copy.51 = bf16[2,4,63,3584]{3,2,1,0:T(8,128)(2,1)} copy(bf16[2,4,63,3584]{3,2,0,1:T(8,128)(2,1)} %bitcast.39) | data formatting | bytes 7225344 | tf_op jit(solution)/shard_map/transpose | solution.py:96
  62.9 5.5 %reshape.94 = bf16[504,3584]{1,0:T(8,128)(2,1)} reshape(bf16[2,4,63,3584]{3,2,1,0:T(8,128)(2,1)} %copy.51) | data formatting | bytes 7225344 | tf_op jit(solution)/shard_map/reshape | solution.py:96
  68.4 12.2 %fusion.3 = bf16[504,2048]{1,0:T(8,128)(2,1)S(1)} fusion(bf16[504,3584]{1,0:T(8,128)(2,1)} %reshape.94, bf16[1,2048,3584]{2,1,0:T(8,128)(2,1)} %param.6), kind=kOutput, calls=%fused_computation.3 | convolution fusion | flops 7399784448 | bytes 20357120 | tf_op jit(solution)/shard_map/dot_general | solution.py:98
  80.6 28.2 %fusion = bf16[256,2048]{1,0:T(8,128)(2,1)S(1)} fusion(bf16[504,2048]{1,0:T(8,128)(2,1)S(1)} %fusion.3), kind=kCustom, calls=%all-reduce-scatter | all-reduce-scatter fusion | flops 1048577 | bytes 3113472
  108.8 2.4 collective-permute-start
  111.3 10.0 %all-gather.2 = s32[4,112,2]{1,2,0:T(2,128)S(1)} all-gather(s32[1,112,2]{1,2,0:T(2,128)S(1)} %bitcast.45), channel_id=2, replica_groups=mesh['rep'=4,'exp'=4,'shard'=2] {'rep'}, dimensions={0}, use_global_device_ids=true | all-gather | bytes 4480 | tf_op jit(solution)/shard_map/all_gather | solution.py:77
  121.5 4.8 %reduce-window.14 = s32[4,4,2,128]{3,2,1,0:T(2,128)S(1)} reduce-window(s32[4,4,2,128]{3,2,1,0:T(2,128)S(1)} %reshape.97, s32[]{:T(128)} %constant.14.clone.1), window={size=1x1x1x128 pad=0_0x0_0x0_0x127_0}, to_apply=%region_1.2 | reduce-window | flops 520192 | bytes 32772 | tf_op jit(solution)/shard_map/reduce-window
  129.6 1.2 reshape.95
  130.9 3.7 %all-to-all-start.1 = ((bf16[4,63,2048]{2,1,0:T(8,128)(2,1)}), bf16[4,63,2048]{2,1,0:T(8,128)(2,1)S(1)}, u32[]{:S(2)}, u32[]{:S(2)}) async-start(bf16[4,63,2048]{2,1,0:T(8,128)(2,1)} %reshape.95), calls=%async_computation.1 | async-start | bytes 2097152 | tf_op jit(solution)/shard_map/all_to_all | solution.py:106
  135.0 3.3 convolution_convert_fusion
  138.4 5.1 %reshape.89 = bf16[4,4,63,2048]{3,2,1,0:T(8,128)(2,1)} reshape(bf16[4,252,2048]{2,1,0:T(8,128)(2,1)} %convolution_convert_fusion) | data formatting | bytes 8257536 | tf_op jit(solution)/shard_map/reshape | solution.py:87
  143.5 7.4 %copy.44 = bf16[4,4,63,2048]{3,1,2,0:T(4,128)(2,1)} copy(bf16[4,4,63,2048]{3,2,0,1:T(8,128)(2,1)} %bitcast.38) | data formatting | bytes 8257536 | tf_op jit(solution)/shard_map/transpose | solution.py:87
  150.9 6.3 %broadcast_in_dim.8 = bf16[4,2,4,63,2048]{4,2,3,1,0:T(4,128)(2,1)} broadcast(bf16[4,4,63,2048]{3,1,2,0:T(4,128)(2,1)} %copy.44), dimensions={0,2,3,4} | broadcast | bytes 12386304 | tf_op jit(solution)/shard_map/broadcast_in_dim | solution.py:88
  157.2 4.9 %all-to-all-start = ((bf16[8,4,63,2048]{3,1,2,0:T(4,128)(2,1)}), bf16[8,4,63,2048]{3,1,2,0:T(4,128)(2,1)}, u32[]{:S(2)}, u32[]{:S(2)}) async-start(bf16[8,4,63,2048]{3,1,2,0:T(4,128)(2,1)} %bitcast.37), calls=%async_computation | async-start | bytes 16515072 | tf_op jit(solution)/shard_map/all_to_all | solution.py:90
  162.2 2.2 slice.31
  164.4 79.3 %all-gather.7.cloned.1.call-done.refs_1_ = bf16[4,504,2688]{2,1,0:T(8,128)(2,1)} async-done(((bf16[1,504,2688]{2,1,0:T(8,128)(2,1)}), bf16[4,504,2688]{2,1,0:T(8,128)(2,1)}) %all-gather.7.cloned.1.call-update) | async-done | bytes 10838032 | tf_op jit(solution)/shard_map/all_gather | solution.py:79
  247.4 6.5 %all-to-all-done = bf16[8,4,63,2048]{3,1,2,0:T(4,128)(2,1)} async-done(((bf16[8,4,63,2048]{3,1,2,0:T(4,128)(2,1)}), bf16[8,4,63,2048]{3,1,2,0:T(4,128)(2,1)}, u32[]{:S(2)}, u32[]{:S(2)}) %all-to-all-start) | async-done | bytes 8257568 | tf_op jit(solution)/shard_map/all_to_all | solution.py:90
  254.0 13.7 %copy.46 = bf16[4,504,2048]{1,2,0:T(8,128)(2,1)} copy(bf16[4,504,2048]{2,0,1:T(4,128)(2,1)} %bitcast.9) | data formatting | bytes 16515072 | tf_op jit(solution)/shard_map/reshape | solution.py:91
  267.7 33.2 %shard_map.59.refs_2_ = bf16[1,2048,3584]{2,1,0:T(8,128)(2,1)} custom-call(bf16[4,2048,504]{2,1,0:T(8,128)(2,1)} %bitcast.35, bf16[4,504,2688]{2,1,0:T(8,128)(2,1)} %all-gather.7.cloned.1.call-done.refs_1_), custom_call_target="tpu_custom_call" | custom-call | flops 22196256768 | bytes 30105600 | tf_op jit(solution)/shard_map/pallas_call | solution.py:45
  300.9 13.8 %all-gather.9.cloned.1.call-done.refs_1_ = bf16[4,504,896]{2,1,0:T(8,128)(2,1)} async-done(((bf16[1,504,896]{2,1,0:T(8,128)(2,1)}), bf16[4,504,896]{2,1,0:T(8,128)(2,1)}) %all-gather.9.cloned.1.call-update) | async-done | bytes 3612688 | tf_op jit(solution)/shard_map/all_gather | solution.py:81
  314.7 13.0 %shard_map.60 = bf16[1,2048,3584]{2,1,0:T(8,128)(2,1)} custom-call(bf16[4,2048,504]{2,1,0:T(8,128)(2,1)} %bitcast.36, bf16[4,504,896]{2,1,0:T(8,128)(2,1)} %all-gather.9.cloned.1.call-done.refs_1_, bf16[1,2048,3584]{2,1,0:T(8,128)(2,1)} %shard_map.59.refs_2_), custom_call_target="tpu_custom_call", output_to_operand_aliasing={{}: (2, {})} | custom-call | flops 7398752256 | bytes 15540224 | tf_op jit(solution)/shard_map/pallas_call | solution.py:45
  (55 shorter events, 7.7 us)
Async XLA Ops:
  7.2 46.5 %all-gather.11.cloned.1.call-start = ((), (), s32[]{:S(2)}) async-start(), calls=%async_computation.4 | async-start | bytes 2293760 | tf_op jit(solution)/shard_map/all_gather | solution.py:76
  7.9 235.9 %all-gather.7.cloned.1.call-start = ((), (), s32[]{:S(2)}) async-start(), calls=%async_computation.2 | async-start | bytes 13547520 | tf_op jit(solution)/shard_map/all_gather | solution.py:79
  68.4 42.9 %copy-start.1 = (s32[112,2]{0,1:T(2,128)S(1)}, s32[112,2]{0,1:T(2,128)}, u32[]{:S(2)}) copy-start(s32[112,2]{0,1:T(2,128)} %param.5) | copy-start | bytes 2692
  68.4 58.4 %copy-start.2 = (u32[32]{0:T(128)S(1)}, u32[32]{0:T(128)}, u32[]{:S(2)}) copy-start(u32[32]{0:T(128)} %constant.27) | copy-start | bytes 388
  108.8 19.3 %collective-permute-start = (bf16[4,2048]{1,0:T(4,128)(2,1)S(1)}, bf16[4,2048]{1,0:T(4,128)(2,1)S(1)}, u32[]{:S(2)}, u32[]{:S(2)}) collective-permute-start(bf16[4,2048]{1,0:T(4,128)(2,1)S(1)} %slice.37), channel_id=1, source_target_pairs={{0,1},{2,3},{4,5},{6,7},{8,9},{10,11},{12,13},{14,15},{16,17},{18,... | collective-permute-start | bytes 49160
  129.6 5.4 %copy-start = (bf16[448,2048]{1,0:T(8,128)(2,1)S(1)}, bf16[448,2048]{1,0:T(8,128)(2,1)}, u32[]{:S(2)}) copy-start(bf16[448,2048]{1,0:T(8,128)(2,1)} %all-gather.11.cloned.1.call-done) | copy-start | bytes 5505028
  130.9 20.1 %all-to-all-start.1 = ((bf16[4,63,2048]{2,1,0:T(8,128)(2,1)}), bf16[4,63,2048]{2,1,0:T(8,128)(2,1)S(1)}, u32[]{:S(2)}, u32[]{:S(2)}) async-start(bf16[4,63,2048]{2,1,0:T(8,128)(2,1)} %reshape.95), calls=%async_computation.1 | async-start | bytes 2097152 | tf_op jit(solution)/shard_map/all_to_all | solution.py:106
  157.2 96.7 %all-to-all-start = ((bf16[8,4,63,2048]{3,1,2,0:T(4,128)(2,1)}), bf16[8,4,63,2048]{3,1,2,0:T(4,128)(2,1)}, u32[]{:S(2)}, u32[]{:S(2)}) async-start(bf16[8,4,63,2048]{3,1,2,0:T(4,128)(2,1)} %bitcast.37), calls=%async_computation | async-start | bytes 16515072 | tf_op jit(solution)/shard_map/all_to_all | solution.py:90
  162.2 152.5 %all-gather.9.cloned.1.call-start = ((), (), s32[]{:S(2)}) async-start(), calls=%async_computation.3 | async-start | bytes 4515840 | tf_op jit(solution)/shard_map/all_gather | solution.py:81
Sparse Core Ops, SparseCore 0:
  9.5 44.0 all-gather.10
  55.2 188.5 all-gather.6
  245.4 69.2 all-gather.8

commit v2 on v1

--- a/solution.py
+++ b/solution.py
@@ -60,6 +60,11 @@
     )(*operands)
 
 
+def widest(columns, least):
+    sizes = [least * u for u in range(1, columns // least + 1) if columns % (least * u) == 0]
+    return max(c for c in sizes if c <= max(least, 1024))
+
+
 def body(tokens, routes, gate_weight, gate_cotangent):
     experts = lax.axis_size("exp")
     shards = lax.axis_size("shard")
@@ -70,15 +75,16 @@
     slot_cap = rows // (experts * shards)
     weight = gate_weight[0]
     units = hidden // 128
-    width = 128 * max(u for u in range(1, units + 1) if units % u == 0 and u <= max(1, units // 4))
+    width = 128 * max(u for u in range(1, units + 1) if units % u == 0 and u <= max(1, units // 7))
     split = hidden - width
 
-    all_tokens = lax.all_gather(tokens[None], "rep", axis=0, tiled=True)
+    first_all = lax.all_gather(gate_cotangent[:, :, :split], "rep", axis=0, tiled=True)
     all_routes = lax.all_gather(routes[None], "rep", axis=0, tiled=True)
-    first_part, all_tokens = lax.optimization_barrier((gate_cotangent[:, :, :split], all_tokens))
-    first_all = lax.all_gather(first_part, "rep", axis=0, tiled=True)
-    last_part, first_all = lax.optimization_barrier((gate_cotangent[:, :, split:], first_all))
-    last_all = lax.all_gather(last_part, "rep", axis=0, tiled=True)
+    half = tokens.shape[0] // 2
+    upper = lax.all_gather(tokens[None, :half], "rep", axis=0, tiled=True)
+    lower, upper = lax.optimization_barrier((tokens[None, half:], upper))
+    lower = lax.all_gather(lower, "rep", axis=0, tiled=True)
+    all_tokens = jnp.concatenate([upper, lower], axis=1)
 
     placing_all = jax.vmap(lambda r: slot_matrix(r, experts, slot_cap))(all_routes).astype(jnp.bfloat16)
     outgoing = lax.dot_general(
@@ -87,9 +93,8 @@
     outgoing = outgoing.reshape(replicas, experts, slot_cap, features).swapaxes(0, 1)
     copies = jnp.broadcast_to(outgoing[:, None], (experts, shards, replicas, slot_cap, features))
     copies = copies.reshape(experts * shards, replicas, slot_cap, features)
+    copies, cotangent = lax.optimization_barrier((copies, cotangent))
     arrived = lax.all_to_all(copies, ("exp", "shard"), split_axis=0, concat_axis=0, tiled=True)
-    gathered = arrived.swapaxes(0, 1).reshape(replicas, rows, features)
-    lifted = gathered.swapaxes(1, 2)
 
     placing = slot_matrix(routes, experts, slot_cap).astype(jnp.bfloat16)
     blocks = cotangent.reshape(experts, shards, slot_cap, hidden)
@@ -102,14 +107,20 @@
         scatter_dimension=0,
         tiled=True,
     )
+    arrived, summed = lax.optimization_barrier((arrived, summed))
+    gathered = arrived.swapaxes(0, 1).reshape(replicas, rows, features)
+    lifted = gathered.swapaxes(1, 2)
     slot_grad = summed.reshape(experts, slot_cap, features)
     returned = lax.all_to_all(slot_grad, "exp", split_axis=0, concat_axis=0, tiled=True)
     token_grad = jnp.dot(
         placing.T, returned.reshape(-1, features), preferred_element_type=jnp.float32
     ).astype(jnp.bfloat16)
 
-    lifted, token_grad = lax.optimization_barrier((lifted, token_grad))
-    weight_grad = grad_columns(lifted, first_all, None, hidden, 0, width)
+    last_part, first_all, lifted = lax.optimization_barrier(
+        (gate_cotangent[:, :, split:], first_all, lifted)
+    )
+    last_all = lax.all_gather(last_part, "rep", axis=0, tiled=True)
+    weight_grad = grad_columns(lifted, first_all, None, hidden, 0, widest(split, width))
     weight_grad = grad_columns(lifted, last_all, weight_grad, hidden, split, width)
     return (token_grad, weight_grad)
 

time: 335 us -> 325 us (0.970)
  waiting for transfers between devices: 142 us -> 9.9 us
  blocking collectives: 38.2 us -> 169 us
  local copies, waits for them, and re-layouts: 58.2 us -> 53.2 us
  Pallas kernels: 46.2 us -> 42.6 us
    all_gather x2 -> x1, waiting for transfers between devices: 121 us -> 0.01 us  [body(): lax.all_gather(gate_cotangent[:, :, :split], 'rep', axis=0, tiled=True)]
    all_gather x0 -> x2, blocking collectives: none -> 68.2 us  [the longest x1 34.2 us: body(): lower = lax.all_gather(lower, 'rep', axis=0, tiled=True)]
    unnamed x1, blocking collectives: 28.2 us -> 88.3 us
    all_to_all x1, waiting for transfers between devices: 6.5 us -> 0.01 us  [body(): lax.all_to_all(copies, ('exp', 'shard'), split_axis=0, concat_axis=0, til...]
    reshape x0 -> x1, local copies, waits for them, and re-layouts: none -> 4.91 us  [body(): blocks = cotangent.reshape(experts, shards, slot_cap, hidden)]
    another operation x10 -> x9, local copies, waits for them, and re-layouts: 5.38 us -> 0.49 us  [the longest x1 4.93 us: body(): blocks = cotangent.reshape(experts, shards, slot_cap, hidden)]
    all_gather x1, waiting for transfers between devices: 13.8 us -> 9.86 us  [body(): last_all = lax.all_gather(last_part, 'rep', axis=0, tiled=True)]
    pallas_call x2, Pallas kernels: 46.2 us -> 42.6 us  [grad_columns(): pl.pallas_call(grad_kernel, grid=(columns // width, features // tall), in...]
  transfers between devices with their start and end apart: 6 -> 5, of which waited for: 4 -> 1; matrix products, arithmetic and copies ran while one was open for 33% -> 50% of each run, Pallas kernels for 10% -> 10%
where the time goes in v2:
time: 325 us; the launch traced here: 324 us
  blocking collectives  169 us (52%)
  local copies, waits for them, and re-layouts  53.2 us (16%)
  Pallas kernels  42.6 us (13%)
  matrix products  16.4 us (5%)
  between operations  14.9 us (5%)
  starting transfers between devices  10.8 us (3%)
  waiting for transfers between devices  9.9 us (3%)
  other arithmetic  6.69 us (2%)
    unnamed x1, blocking collectives  88.3 us
    pallas_call x2, Pallas kernels, grad_columns(): pl.pallas_call(grad_kernel, grid=(columns // width, features // tall), in...  42.6 us
    all_gather x1, blocking collectives, body(): lower = lax.all_gather(lower, 'rep', axis=0, tiled=True)  34.2 us
    all_gather x1, blocking collectives, body(): upper = lax.all_gather(tokens[None, :half], 'rep', axis=0, tiled=True)  33.9 us
    reshape x1, local copies, waits for them, and re-layouts, body(): gathered = arrived.swapaxes(0, 1).reshape(replicas, rows, features)  13.7 us
    all_gather x1, blocking collectives, body(): all_routes = lax.all_gather(routes[None], 'rep', axis=0, tiled=True)  12.7 us
    dot_general x1, matrix products, body(): lax.dot_general(ordered, weight, (((1,), (1,)), ((), ())), preferred_elem...  12 us
    all_gather x1, waiting for transfers between devices, body(): last_all = lax.all_gather(last_part, 'rep', axis=0, tiled=True)  9.86 us
  transfers between devices with their start and end apart: 5, of which 1 were waited for; matrix products, arithmetic and copies ran while one was open for 50% of the time, Pallas kernels for 10%

profile of v2, /device:TPU:0, one launch (start us, length us, event | category | flops | bytes accessed | tf_op | source)
XLA Modules:
  0.0 323.7 jit_solution(12074504642661063683)
XLA Ops:
  7.2 3.8 %slice.39 = bf16[1,504,3072]{2,1,0:T(8,128)(2,1)} slice(bf16[1,504,3584]{2,1,0:T(8,128)(2,1)} %param.7), slice={[0:1], [0:504], [0:3072]} | slice | bytes 6193152 | tf_op jit(solution)/shard_map/slice | solution.py:81
  11.1 12.7 %all-gather.2 = s32[4,112,2]{1,2,0:T(2,128)S(1)} all-gather(s32[1,112,2]{1,2,0:T(2,128)S(1)} %bitcast.48), channel_id=2, replica_groups=mesh['rep'=4,'exp'=4,'shard'=2] {'rep'}, dimensions={0}, use_global_device_ids=true | all-gather | bytes 4480 | tf_op jit(solution)/shard_map/all_gather | solution.py:82
  24.0 4.8 %reduce-window.16 = s32[4,4,2,128]{3,2,1,0:T(2,128)S(1)} reduce-window(s32[4,4,2,128]{3,2,1,0:T(2,128)S(1)} %reshape.102, s32[]{:T(128)} %constant.14.clone.1), window={size=1x1x1x128 pad=0_0x0_0x0_0x127_0}, to_apply=%region_6.7 | reduce-window | flops 520192 | bytes 32772 | tf_op jit(solution)/shard_map/reduce-window.2
  29.6 33.9 %all-gather.1 = bf16[224,2048]{1,0:T(8,128)(2,1)S(1)} all-gather(bf16[56,2048]{1,0:T(8,128)(2,1)S(1)} %get-tuple-element.24), channel_id=3, replica_groups=mesh['rep'=4,'exp'=4,'shard'=2] {'rep'}, dimensions={0}, use_global_device_ids=true | all-gather | bytes 1146880 | tf_op jit(solution)/shard_map/all_gather | solution.py:84
  63.8 34.2 %all_gather.17 = bf16[4,56,2048]{2,1,0:T(8,128)(2,1)S(1)} all-gather(bf16[1,56,2048]{2,1,0:T(8,128)(2,1)S(1)} %get-tuple-element.12), channel_id=1, replica_groups=mesh['rep'=4,'exp'=4,'shard'=2] {'rep'}, dimensions={0}, use_global_device_ids=true | all-gather | bytes 1146880 | tf_op jit(solution)/shard_map/all_gather | solution.py:86
  98.0 3.3 %convolution_convert_fusion = bf16[4,252,2048]{2,1,0:T(8,128)(2,1)} fusion(bf16[4,56,2048]{2,1,0:T(8,128)(2,1)S(1)} %all_gather.17, bf16[4,56,2048]{2,1,0:T(8,128)(2,1)S(1)} %bitcast.43, s32[4,252,112]{1,2,0:T(8,128)S(1)} %convert_reduce_fusion), kind=kOutput, calls=%fused_computation.2 | convolution fusion | flops 468269312 | bytes 6415360 | tf_op jit(solution)/shard_map/dot_general | solution.py:90
  101.3 5.2 %reshape.94 = bf16[4,4,63,2048]{3,2,1,0:T(8,128)(2,1)} reshape(bf16[4,252,2048]{2,1,0:T(8,128)(2,1)} %convolution_convert_fusion) | data formatting | bytes 8257536 | tf_op jit(solution)/shard_map/reshape | solution.py:93
  106.5 5.4 %copy.48 = bf16[4,4,63,2048]{3,1,2,0:T(4,128)(2,1)S(1)} copy(bf16[4,4,63,2048]{3,2,0,1:T(8,128)(2,1)} %bitcast.40) | data formatting | bytes 8257536 | tf_op jit(solution)/shard_map/transpose | solution.py:93
  111.9 4.1 %broadcast_in_dim.11 = bf16[4,2,4,63,2048]{4,2,3,1,0:T(4,128)(2,1)} broadcast(bf16[4,4,63,2048]{3,1,2,0:T(4,128)(2,1)S(1)} %copy.48), dimensions={0,2,3,4} | broadcast | bytes 12386304 | tf_op jit(solution)/shard_map/broadcast_in_dim | solution.py:94
  116.0 5.0 %all-to-all-start = ((bf16[8,4,63,2048]{3,1,2,0:T(4,128)(2,1)}), bf16[8,4,63,2048]{3,1,2,0:T(4,128)(2,1)}, u32[]{:S(2)}, u32[]{:S(2)}) async-start(bf16[8,4,63,2048]{3,1,2,0:T(4,128)(2,1)} %bitcast.39), calls=%async_computation | async-start | bytes 16515072 | tf_op jit(solution)/shard_map/all_to_all | solution.py:97
  121.0 4.9 %reshape.96 = bf16[4,2,63,3584]{3,2,1,0:T(8,128)(2,1)} reshape(bf16[504,3584]{1,0:T(8,128)(2,1)} %bitcast.42) | data formatting | bytes 7225344 | tf_op jit(solution)/shard_map/reshape | solution.py:100
  125.9 4.1 %copy.49 = bf16[2,4,63,3584]{3,2,1,0:T(8,128)(2,1)} copy(bf16[2,4,63,3584]{3,2,0,1:T(8,128)(2,1)} %bitcast.41) | data formatting | bytes 7225344 | tf_op jit(solution)/shard_map/transpose | solution.py:101
  130.0 4.9 %reshape.97 = bf16[504,3584]{1,0:T(8,128)(2,1)} reshape(bf16[2,4,63,3584]{3,2,1,0:T(8,128)(2,1)} %copy.49) | data formatting | bytes 7225344 | tf_op jit(solution)/shard_map/reshape | solution.py:101
  134.9 12.0 %fusion.3 = bf16[504,2048]{1,0:T(8,128)(2,1)S(1)} fusion(bf16[504,3584]{1,0:T(8,128)(2,1)} %reshape.97, bf16[1,2048,3584]{2,1,0:T(8,128)(2,1)} %param.6), kind=kOutput, calls=%fused_computation.3 | convolution fusion | flops 7399784448 | bytes 20357120 | tf_op jit(solution)/shard_map/dot_general | solution.py:103
  147.0 88.3 %fusion = bf16[256,2048]{1,0:T(8,128)(2,1)S(1)} fusion(bf16[504,2048]{1,0:T(8,128)(2,1)S(1)} %fusion.3), kind=kCustom, calls=%all-reduce-scatter | all-reduce-scatter fusion | flops 1048577 | bytes 3113472
  235.3 2.3 collective-permute-start
  237.9 1.9 slice.38
  241.0 1.2 concatenate.4
  242.5 1.2 reshape.98
  243.8 3.5 %all-to-all-start.1 = ((bf16[4,63,2048]{2,1,0:T(8,128)(2,1)}), bf16[4,63,2048]{2,1,0:T(8,128)(2,1)S(1)}, u32[]{:S(2)}, u32[]{:S(2)}) async-start(bf16[4,63,2048]{2,1,0:T(8,128)(2,1)} %reshape.98), calls=%async_computation.1 | async-start | bytes 2097152 | tf_op jit(solution)/shard_map/all_to_all | solution.py:114
  248.9 13.7 %copy.51 = bf16[4,504,2048]{1,2,0:T(8,128)(2,1)} copy(bf16[4,504,2048]{2,0,1:T(4,128)(2,1)} %bitcast.15) | data formatting | bytes 16515072 | tf_op jit(solution)/shard_map/reshape | solution.py:111
  264.5 33.9 %shard_map.59.refs_2_ = bf16[1,2048,3584]{2,1,0:T(8,128)(2,1)} custom-call(bf16[4,2048,504]{2,1,0:T(8,128)(2,1)} %bitcast.37, bf16[4,504,3072]{2,1,0:T(8,128)(2,1)} %all-gather.6.cloned.1.call-done.refs_1_), custom_call_target="tpu_custom_call" | custom-call | flops 25367150592 | bytes 33226752 | tf_op jit(solution)/shard_map/pallas_call | solution.py:45
  298.3 9.9 %all-gather.8.cloned.1.call-done.refs_1_ = bf16[4,504,512]{2,1,0:T(8,128)(2,1)} async-done(((bf16[1,504,512]{2,1,0:T(8,128)(2,1)}), bf16[4,504,512]{2,1,0:T(8,128)(2,1)}) %all-gather.8.cloned.1.call-update) | async-done | bytes 2064400 | tf_op jit(solution)/shard_map/all_gather | solution.py:122
  308.2 8.7 %shard_map.60 = bf16[1,2048,3584]{2,1,0:T(8,128)(2,1)} custom-call(bf16[4,2048,504]{2,1,0:T(8,128)(2,1)} %bitcast.38, bf16[4,504,512]{2,1,0:T(8,128)(2,1)} %all-gather.8.cloned.1.call-done.refs_1_, bf16[1,2048,3584]{2,1,0:T(8,128)(2,1)} %shard_map.59.refs_2_), custom_call_target="tpu_custom_call", output_to_operand_aliasing={{}: (2, {})} | custom-call | flops 4227858432 | bytes 12419072 | tf_op jit(solution)/shard_map/pallas_call | solution.py:45
  (55 shorter events, 5.8 us)
Async XLA Ops:
  7.2 3.9 %copy-start.1 = (s32[112,2]{0,1:T(2,128)S(1)}, s32[112,2]{0,1:T(2,128)}, u32[]{:S(2)}) copy-start(s32[112,2]{0,1:T(2,128)} %param.5) | copy-start | bytes 2692
  7.2 22.4 %copy-start = (bf16[112,2048]{1,0:T(8,128)(2,1)S(1)}, bf16[112,2048]{1,0:T(8,128)(2,1)}, u32[]{:S(2)}) copy-start(bf16[112,2048]{1,0:T(8,128)(2,1)} %param.4) | copy-start | bytes 1376260
  7.2 255.4 %all-gather.6.cloned.1.call-start = ((), (), s32[]{:S(2)}) async-start(), calls=%async_computation.2 | async-start | bytes 15482880 | tf_op jit(solution)/shard_map/all_gather | solution.py:81
  116.0 126.5 %all-to-all-start = ((bf16[8,4,63,2048]{3,1,2,0:T(4,128)(2,1)}), bf16[8,4,63,2048]{3,1,2,0:T(4,128)(2,1)}, u32[]{:S(2)}, u32[]{:S(2)}) async-start(bf16[8,4,63,2048]{3,1,2,0:T(4,128)(2,1)} %bitcast.39), calls=%async_computation | async-start | bytes 16515072 | tf_op jit(solution)/shard_map/all_to_all | solution.py:97
  147.0 92.8 %copy-start.2 = (u32[32]{0:T(128)S(1)}, u32[32]{0:T(128)}, u32[]{:S(2)}) copy-start(u32[32]{0:T(128)} %constant.27) | copy-start | bytes 388
  235.3 5.7 %collective-permute-start = (bf16[4,2048]{1,0:T(4,128)(2,1)S(1)}, bf16[4,2048]{1,0:T(4,128)(2,1)S(1)}, u32[]{:S(2)}, u32[]{:S(2)}) collective-permute-start(bf16[4,2048]{1,0:T(4,128)(2,1)S(1)} %slice.45), channel_id=1, source_target_pairs={{0,1},{2,3},{4,5},{6,7},{8,9},{10,11},{12,13},{14,15},{16,17},{18,... | collective-permute-start | bytes 49160
  243.8 19.3 %all-to-all-start.1 = ((bf16[4,63,2048]{2,1,0:T(8,128)(2,1)}), bf16[4,63,2048]{2,1,0:T(8,128)(2,1)S(1)}, u32[]{:S(2)}, u32[]{:S(2)}) async-start(bf16[4,63,2048]{2,1,0:T(8,128)(2,1)} %reshape.98), calls=%async_computation.1 | async-start | bytes 2097152 | tf_op jit(solution)/shard_map/all_to_all | solution.py:114
  247.3 60.9 %all-gather.8.cloned.1.call-start = ((), (), s32[]{:S(2)}) async-start(), calls=%async_computation.3 | async-start | bytes 2580480 | tf_op jit(solution)/shard_map/all_gather | solution.py:122
Sparse Core Ops, SparseCore 0:
  11.2 247.0 all-gather.5
  262.8 45.3 all-gather.7
